TPU v7x, 32 devices: a whole 2x2x4 slice. The times are simulated.
32 devices in a mesh: seq: 4 (over x, core), tp: 8 (over z, y).
Axes of the slice: x: 2, y: 2, z: 4, core: 2. Of those that a mesh axis runs over, the one named last changes fastest.
Arguments:
- vit_input: bfloat16 [2048, 1280], P(('seq', 'tp')), may hold values from -6 to 6
- image_lengths: int32 [4, 2], P('seq'), may hold values from 1 to 96, 128 in all within a row
- positions: int32 [512], replicated, may hold values from 0 to 511, each once
- vit_ln_gain: float32 [1280], replicated, may hold values from 0.25 to 1.75
- w_qkv: bfloat16 [1280, 3, 1280], P(None, None, 'tp'), may hold values from -0.15625 to 0.15625
- w_proj: bfloat16 [1280, 1280], P('tp'), may hold values from -0.15625 to 0.15625
- merger_ln_gain: float32 [1280], replicated, may hold values from 0.25 to 1.75
- merger_w1: bfloat16 [5120, 5120], P(None, 'tp'), may hold values from -0.078125 to 0.078125
- merger_w2: bfloat16 [5120, 8192], P('tp'), may hold values from -0.36336105 to 0.36336105
- norm_gain: float32 [8192], P('seq'), may hold values from 0.25 to 1.75
- gate_up_weight: bfloat16 [8192, 2, 29568], P('seq', None, 'tp'), may hold values from -0.0625 to 0.0625
- down_weight: bfloat16 [29568, 8192], P('tp', 'seq'), may hold values from -0.125 to 0.125
Outputs:
- mixed: bfloat16 [512, 8192], P('tp', 'seq')
Inputs may be any that keep to these rules, and one draw needn't show every extreme that they name: `image_lengths`: each row sums to 128. `positions`: a permutation: every slot once.
All inputs are finite; a program needn't handle non-finite values.
Results may differ from a plain program's by a relative error of at most 0.038.
Values may be sent and summed in bfloat16 or wider, within the bound.
A program may use at most 128 MiB of HBM per device.

v0:
```python
import jax
import jax.numpy as jnp
from jax import lax
from jax.sharding import PartitionSpec as P

D = 8192
HD = 80


def layer_norm(values, gain):
    mean = jnp.mean(values, axis=-1, keepdims=True)
    centered = values - mean
    variance = jnp.mean(centered * centered, axis=-1, keepdims=True)
    return centered * lax.rsqrt(variance + 1e-06) * gain


def image_ids(lengths, count):
    image_ends = jnp.cumsum(lengths) * 4
    patch_index = jnp.arange(count, dtype=jnp.int32)
    return jnp.sum((patch_index[:, None] >= image_ends[None, :]).astype(jnp.int32), axis=1)


def attend(query, keys, values, image_index):
    scores = jnp.einsum("qhe,khe->hqk", query, keys, preferred_element_type=jnp.float32) * HD ** (
        -0.5
    )
    same_image = image_index[:, None] == image_index[None, :]
    scores = jnp.where(same_image[None], scores, -1e30)
    top = jnp.max(scores, axis=-1, keepdims=True)
    expo = jnp.exp(scores - top)
    weights = (expo / jnp.sum(expo, axis=-1, keepdims=True)).astype(jnp.bfloat16)
    output = jnp.einsum("hqk,khe->qhe", weights, values, preferred_element_type=jnp.float32)
    return output.astype(jnp.bfloat16)


def slot_sources(positions):
    count = positions.shape[0]
    return jnp.zeros((count,), jnp.int32).at[positions].set(jnp.arange(count, dtype=jnp.int32))


def local(
    vit_input,
    image_lengths,
    positions,
    vit_ln_gain,
    w_qkv,
    w_proj,
    merger_ln_gain,
    merger_w1,
    merger_w2,
    norm_gain,
    gate_up_weight,
    down_weight,
):
    tp_size = lax.axis_size("tp")
    own_patches = vit_input.shape[0]
    patch_width = vit_input.shape[1]
    head_cols = w_qkv.shape[2]
    local_heads = head_cols // HD
    normed_patches = layer_norm(vit_input.astype(jnp.float32), vit_ln_gain).astype(jnp.bfloat16)
    w_qkv_flat = w_qkv.reshape(patch_width, 3 * head_cols)
    projected = jnp.dot(
        lax.all_gather(normed_patches, "tp", axis=0, tiled=True),
        w_qkv_flat,
        preferred_element_type=jnp.float32,
    ).astype(jnp.bfloat16)
    group_patches = projected.shape[0]
    projected = projected.reshape(group_patches, 3, local_heads, HD)
    image_index = image_ids(image_lengths[0], group_patches)
    attended = attend(projected[:, 0], projected[:, 1], projected[:, 2], image_index).reshape(
        group_patches, head_cols
    )
    picked = attended
    attn_sum = lax.psum_scatter(
        jnp.dot(picked, w_proj, preferred_element_type=jnp.float32).astype(jnp.bfloat16),
        "tp",
        scatter_dimension=0,
        tiled=True,
    ).astype(jnp.float32)
    vit_out = vit_input.astype(jnp.float32) + attn_sum
    own_tokens = own_patches // 4
    merged_in = (
        layer_norm(vit_out, merger_ln_gain)
        .astype(jnp.bfloat16)
        .reshape(own_tokens, 4 * patch_width)
    )
    expanded = jax.nn.gelu(
        jnp.dot(
            lax.all_gather(merged_in, "tp", axis=0, tiled=True),
            merger_w1,
            preferred_element_type=jnp.float32,
        ),
        approximate=False,
    ).astype(jnp.bfloat16)
    picked = expanded
    vis_rows = lax.psum_scatter(
        jnp.dot(picked, merger_w2, preferred_element_type=jnp.float32).astype(jnp.bfloat16),
        "tp",
        scatter_dimension=0,
        tiled=True,
    )
    group_rows = lax.all_gather(vis_rows, "tp", axis=0, tiled=True)
    all_tokens = lax.all_to_all(group_rows, "seq", split_axis=1, concat_axis=0, tiled=True)
    seq_rows = all_tokens.shape[0]
    seq_tokens = jnp.take(all_tokens, slot_sources(positions), axis=0)
    token_values = seq_tokens.astype(jnp.float32)
    row_squares = lax.psum(jnp.sum(token_values * token_values, axis=1), "seq")
    inverse_rms = lax.rsqrt(row_squares / D + 1e-06)
    normed = (token_values * inverse_rms[:, None] * norm_gain).astype(jnp.bfloat16)
    slice_width = seq_tokens.shape[1]
    hidden_width = gate_up_weight.shape[2]
    weight_flat = gate_up_weight.reshape(slice_width, 2 * hidden_width)
    out_rows = seq_rows // tp_size
    picked = normed
    gate_up = lax.psum_scatter(
        jnp.dot(picked, weight_flat, preferred_element_type=jnp.float32).astype(jnp.bfloat16),
        "seq",
        scatter_dimension=0,
        tiled=True,
    ).astype(jnp.float32)
    hidden = (jax.nn.silu(gate_up[:, :hidden_width]) * gate_up[:, hidden_width:]).astype(
        jnp.bfloat16
    )
    terms = jnp.dot(
        lax.all_gather(hidden, "seq", axis=0, tiled=True),
        down_weight,
        preferred_element_type=jnp.float32,
    )
    down_sum = lax.psum_scatter(
        terms.astype(jnp.bfloat16), "tp", scatter_dimension=0, tiled=True
    ).astype(jnp.float32)
    residual = lax.dynamic_slice_in_dim(token_values, lax.axis_index("tp") * out_rows, out_rows, 0)
    return (residual + down_sum).astype(jnp.bfloat16)


def solution(mesh):
    return jax.shard_map(
        local,
        mesh=mesh,
        in_specs=(
            P(("seq", "tp"), None),
            P("seq", None),
            P(),
            P(),
            P(None, None, "tp"),
            P("tp", None),
            P(),
            P(None, "tp"),
            P("tp", None),
            P("seq"),
            P("seq", None, "tp"),
            P("tp", "seq"),
        ),
        out_specs=P("tp", "seq"),
        check_vma=False,
    )
```

profile of v0, /device:TPU:0, one launch (start us, length us, event | category | flops | bytes accessed | tf_op | source)
XLA Modules:
  0.0 574.5 jit_solution(16875621755444361467)
XLA Ops:
  6.5 1.1 convert_reduce_fusion
  7.7 1.1 fusion.11
  8.8 1.7 fusion.13
  10.5 0.0 all-gather.5.cloned.1.call-update
  10.6 0.0 reduce-scatter.7.cloned.1.call-start
  10.6 0.8 reduce-window.8
  11.5 0.1 fusion.60
  11.5 0.2 broadcast_compare_fusion
  11.8 43.5 %all-gather.5.cloned.1.call-done = bf16[512,1280]{1,0:T(8,128)(2,1)} async-done(((bf16[64,1280]{1,0:T(8,128)(2,1)}), bf16[512,1280]{1,0:T(8,128)(2,1)}) %all-gather.5.cloned.1.call-update) | async-done | bytes 1310736 | tf_op jit(solution)/shard_map/all_gather | solution.py:63
  55.3 2.1 convolution_convert_fusion.4
  57.4 1.0 fusion.101
  58.4 1.2 convolution_convert_fusion.5
  59.7 1.6 convolution_convert_fusion.2
  61.3 0.0 reduce-scatter.7.cloned.1.call-update
  61.3 0.0 all-gather.7.cloned.1.call-start
  61.4 64.1 %reduce-scatter.7.cloned.1.call-done = bf16[64,1280]{1,0:T(8,128)(2,1)} async-done(((bf16[512,1280]{1,0:T(8,128)(2,1)}), bf16[64,1280]{1,0:T(8,128)(2,1)}) %reduce-scatter.7.cloned.1.call-update) | async-done | bytes 163856 | tf_op jit(solution)/shard_map/reduce_scatter | solution.py:74
  125.5 1.1 fusion.25
  126.5 1.1 multiply_reduce_fusion.1
  127.7 1.0 multiply_convert_fusion.2
  128.7 0.8 reshape.111
  129.5 0.0 all-gather.7.cloned.1.call-update
  129.5 0.0 reduce-scatter.9.cloned.1.call-start
  129.6 40.7 %all-gather.7.cloned.1.call-done = bf16[128,5120]{1,0:T(8,128)(2,1)} async-done(((bf16[16,5120]{1,0:T(8,128)(2,1)}), bf16[128,5120]{1,0:T(8,128)(2,1)}) %all-gather.7.cloned.1.call-update) | async-done | bytes 1310736 | tf_op jit(solution)/shard_map/all_gather | solution.py:89
  170.3 11.2 %convolution_convert_fusion.1 = bf16[128,8192]{1,0:T(8,128)(2,1)} fusion(bf16[640,8192]{1,0:T(8,128)(2,1)} %param.20, bf16[128,5120]{1,0:T(8,128)(2,1)} %all-gather.7.cloned.1.call-done, bf16[5120,640]{1,0:T(8,128)(2,1)} %param.19), kind=kOutput, calls=%fused_computation.4 | convolution fusion | flops 2187411456 | bytes 20447232 | tf_op jit(solution)/shard_map/dot_general | solution.py:97
  181.5 0.0 all-gather.9.cloned.1.call-start
  181.5 68.1 %reduce-scatter.9.cloned.1.call-done = bf16[16,8192]{1,0:T(8,128)(2,1)} async-done(((bf16[128,8192]{1,0:T(8,128)(2,1)}), bf16[16,8192]{1,0:T(8,128)(2,1)}) %reduce-scatter.9.cloned.1.call-update) | async-done | bytes 262160 | tf_op jit(solution)/shard_map/reduce_scatter | solution.py:96
  249.7 50.2 %all-gather.9.cloned.1.call-done = bf16[128,8192]{1,0:T(8,128)(2,1)} async-done(((bf16[16,8192]{1,0:T(8,128)(2,1)}), bf16[128,8192]{1,0:T(8,128)(2,1)}) %all-gather.9.cloned.1.call-update) | async-done | bytes 2097168 | tf_op jit(solution)/shard_map/all_gather | solution.py:102
  299.8 3.1 copy.24
  303.0 3.7 all-to-all-start
  306.7 0.0 reduce-scatter.13.cloned.1.call-start
  306.8 2.4 scatter_custom_fusion
  309.3 23.1 %all-to-all-done = bf16[128,4,2048]{2,0,1:T(8,128)(2,1)S(1)} async-done(((bf16[128,4,2048]{2,0,1:T(8,128)(2,1)}), bf16[128,4,2048]{2,0,1:T(8,128)(2,1)S(1)}, u32[]{:S(2)}, u32[]{:S(2)}) %all-to-all-start) | async-done | bytes 2097184 | tf_op jit(solution)/shard_map/all_to_all | solution.py:103
  332.4 3.3 gather_fusion
  335.7 2.4 multiply_reduce_fusion
  338.1 5.9 %psum.7 = f32[512]{0:T(512)S(1)} all-reduce(f32[512]{0:T(512)S(1)} %multiply_reduce_fusion), channel_id=1, replica_groups=mesh['seq'=4,'tp'=8] {'seq'}, use_global_device_ids=true, to_apply=%region_12.13 | all-reduce | flops 512 | bytes 4096 | tf_op jit(solution)/shard_map/psum | solution.py:107
  344.1 23.2 %convolution_convert_fusion = bf16[512,7392]{0,1:T(8,128)(2,1)} fusion(bf16[2048,7392]{0,1:T(8,128)(2,1)} %bitcast.59, f32[2048]{0:T(1024)S(1)} %copy-done.7, f32[512]{0:T(512)S(1)} %add_rsqrt_fusion, bf16[512,2048]{1,0:T(8,128)(2,1)S(1)} %copy-done.2, pred[512]{0:T(512)(128)(4,1)S(1)} %compare_and_fusion), kind=kOutput, calls=%fused_computation.3 | convolution fusion | flops 15511175168 | bytes 39954944 | tf_op jit(solution)/shard_map/dot_general | solution.py:116
  367.2 10.1 %copy.20 = bf16[512,7392]{1,0:T(8,128)(2,1)} copy(bf16[512,7392]{0,1:T(8,128)(2,1)} %convolution_convert_fusion) | data formatting | bytes 15138816
  377.4 0.0 all-gather.11.cloned.1.call-start
  377.5 65.9 %reduce-scatter.13.cloned.1.call-done = bf16[128,7392]{1,0:T(8,128)(2,1)} async-done(((bf16[512,7392]{1,0:T(8,128)(2,1)}), bf16[128,7392]{1,0:T(8,128)(2,1)}) %reduce-scatter.13.cloned.1.call-update) | async-done | bytes 1892368
  443.4 3.9 copy.21
  447.3 1.8 convert_element_type.76
  449.1 1.4 fusion.4
  450.5 0.0 reduce-scatter.11.cloned.1.call-start
  450.6 32.7 %all-gather.11.cloned.1.call-done = bf16[512,3696]{0,1:T(8,128)(2,1)} async-done(((bf16[128,3696]{0,1:T(8,128)(2,1)}), bf16[512,3696]{0,1:T(8,128)(2,1)}) %all-gather.11.cloned.1.call-update) | async-done | bytes 3784720 | tf_op jit(solution)/shard_map/all_gather | solution.py:125
  483.3 13.8 %convolution_convert_fusion.3 = bf16[512,2048]{1,0:T(8,128)(2,1)} fusion(bf16[512,3696]{0,1:T(8,128)(2,1)} %all-gather.11.cloned.1.call-done, bf16[3696,2048]{1,0:T(8,128)(2,1)} %param.23), kind=kOutput, calls=%fused_computation.8 | convolution fusion | flops 7752122368 | bytes 21020672 | tf_op jit(solution)/shard_map/dot_general | solution.py:124
  497.1 2.3 fusion.100
  499.4 66.4 %reduce-scatter.11.cloned.1.call-done = bf16[64,2048]{1,0:T(8,128)(2,1)} async-done(((bf16[512,2048]{1,0:T(8,128)(2,1)}), bf16[64,2048]{1,0:T(8,128)(2,1)}) %reduce-scatter.11.cloned.1.call-update) | async-done | bytes 262160 | tf_op jit(solution)/shard_map/reduce_scatter | solution.py:129
  565.8 1.9 add_convert_fusion
  (33 shorter events, 0.2 us)
Async XLA Ops:
  6.5 48.7 %copy-start = (bf16[1280,3,160]{0,2,1:T(8,128)(2,1)S(1)}, bf16[1280,3,160]{0,2,1:T(8,128)(2,1)}, u32[]{:S(2)}) copy-start(bf16[1280,3,160]{0,2,1:T(8,128)(2,1)} %param.16) | copy-start | bytes 3686404
  6.5 48.7 %all-gather.5.cloned.1.call-start = ((), (), s32[]{:S(2)}) async-start(), calls=%async_computation.5 | async-start | bytes 1474560 | tf_op jit(solution)/shard_map/all_gather | solution.py:63
  10.6 114.9 %reduce-scatter.7.cloned.1.call-start = ((), (), s32[]{:S(2)}) async-start(), calls=%async_computation.6 | async-start | bytes 1474560 | tf_op jit(solution)/shard_map/reduce_scatter | solution.py:74
  58.4 1.3 copy-start.4
  59.7 65.8 %copy-start.3 = (bf16[64,1280]{1,0:T(8,128)(2,1)S(1)}, bf16[64,1280]{1,0:T(8,128)(2,1)}, u32[]{:S(2)}) copy-start(bf16[64,1280]{1,0:T(8,128)(2,1)} %param.12) | copy-start | bytes 491524
  59.7 68.0 %copy-start.5 = (f32[1280]{0:T(1024)S(1)}, f32[1280]{0:T(1024)}, u32[]{:S(2)}) copy-start(f32[1280]{0:T(1024)} %param.18) | copy-start | bytes 15364
  61.3 108.9 %all-gather.7.cloned.1.call-start = ((), (), s32[]{:S(2)}) async-start(), calls=%async_computation.7 | async-start | bytes 1474560 | tf_op jit(solution)/shard_map/all_gather | solution.py:89
  129.5 120.1 %reduce-scatter.9.cloned.1.call-start = ((), (), s32[]{:S(2)}) async-start(), calls=%async_computation.8 | async-start | bytes 2359296 | tf_op jit(solution)/shard_map/reduce_scatter | solution.py:96
  181.5 118.3 %all-gather.9.cloned.1.call-start = ((), (), s32[]{:S(2)}) async-start(), calls=%async_computation.9 | async-start | bytes 2359296 | tf_op jit(solution)/shard_map/all_gather | solution.py:102
  303.0 3.8 copy-start.6
  303.0 29.4 %all-to-all-start = ((bf16[128,4,2048]{2,0,1:T(8,128)(2,1)}), bf16[128,4,2048]{2,0,1:T(8,128)(2,1)S(1)}, u32[]{:S(2)}, u32[]{:S(2)}) async-start(bf16[128,4,2048]{2,0,1:T(8,128)(2,1)} %bitcast.56), calls=%async_computation.2 | async-start | bytes 4194304 | tf_op jit(solution)/shard_map/all_to_all | solution.py:103
  306.7 136.7 %reduce-scatter.13.cloned.1.call-start = ((), (), s32[]{:S(2)}) async-start(), calls=%async_computation.12 | async-start | bytes 9502720
  335.7 8.4 %copy-start.2 = (bf16[512,2048]{1,0:T(8,128)(2,1)S(1)}, bf16[512,2048]{1,0:T(8,128)(2,1)}, u32[]{:S(2)}) copy-start(bf16[512,2048]{1,0:T(8,128)(2,1)} %gather_fusion) | copy-start | bytes 6291460
  335.7 8.4 %copy-start.7 = (f32[2048]{0:T(1024)S(1)}, f32[2048]{0:T(1024)}, u32[]{:S(2)}) copy-start(f32[2048]{0:T(1024)} %param.21) | copy-start | bytes 24580
  377.4 105.9 %all-gather.11.cloned.1.call-start = ((), (), s32[]{:S(2)}) async-start(), calls=%async_computation.10 | async-start | bytes 4730880 | tf_op jit(solution)/shard_map/all_gather | solution.py:125
  450.5 115.3 %reduce-scatter.11.cloned.1.call-start = ((), (), s32[]{:S(2)}) async-start(), calls=%async_computation.11 | async-start | bytes 2359296 | tf_op jit(solution)/shard_map/reduce_scatter | solution.py:129
  497.1 70.6 %copy-start.1 = (bf16[1280,3,160]{0,2,1:T(8,128)(2,1)S(1)}, bf16[1280,3,160]{0,2,1:T(8,128)(2,1)}, u32[]{:S(2)}) copy-start(bf16[1280,3,160]{0,2,1:T(8,128)(2,1)} %param.16) | copy-start | bytes 3686404
Sparse Core Ops, SparseCore 0:
  10.7 44.5 all-gather.4
  61.5 63.9 reduce-scatter.6
  129.6 40.5 all-gather.6
  181.6 67.9 reduce-scatter.8
  251.6 48.1 all-gather.8
  377.5 65.8 reduce-scatter.12
  450.7 32.6 all-gather.10
  497.2 68.5 reduce-scatter.10
where the time goes:
time: 575 us
  waiting for transfers between devices  455 us (79%)
  matrix products  54.1 us (9%)
  local copies, waits for them, and re-layouts  23.8 us (4%)
  other arithmetic  18.2 us (3%)
  between operations  13.7 us (2%)
  blocking collectives  5.94 us (1%)
    reduce_scatter x1, waiting for transfers between devices, local(): lax.psum_scatter(jnp.dot(picked, merger_w2, preferred_element_type=jnp.fl...  68.1 us
    reduce_scatter x1, waiting for transfers between devices, local(): lax.psum_scatter(terms.astype(jnp.bfloat16), 'tp', scatter_dimension=0, t...  66.4 us
    unnamed x9, waiting for transfers between devices  66.1 us
    reduce_scatter x1, waiting for transfers between devices, local(): lax.psum_scatter(jnp.dot(picked, w_proj, preferred_element_type=jnp.float...  64.1 us
    all_gather x1, waiting for transfers between devices, local(): group_rows = lax.all_gather(vis_rows, 'tp', axis=0, tiled=True)  50.2 us
    all_gather x1, waiting for transfers between devices, local(): lax.all_gather(normed_patches, 'tp', axis=0, tiled=True)  43.5 us
    all_gather x1, waiting for transfers between devices, local(): lax.all_gather(merged_in, 'tp', axis=0, tiled=True)  40.7 us
    all_gather x1, waiting for transfers between devices, local(): lax.all_gather(hidden, 'seq', axis=0, tiled=True)  32.7 us
  transfers between devices with their start and end apart: 9, of which 9 were waited for; matrix products, arithmetic and copies ran while one was open for 1% of the time, Pallas kernels for 0%

commit v1 on v0

v1 whole, which is shorter than its diff:
```python
import functools

import jax
import jax.numpy as jnp
from jax import lax
from jax.experimental import pallas as pl
from jax.experimental.pallas import tpu as pltpu
from jax.sharding import PartitionSpec as P

D = 8192
HD = 80
MESH = pl.DeviceIdType.MESH
VM = pl.BlockSpec(memory_space=pltpu.VMEM)


def factors(n):
    minor = max(d for d in range(1, n + 1) if n % d == 0 and d * d <= n)
    return n // minor, minor


def greet(axis, peers):
    barrier = pltpu.get_barrier_semaphore()
    for peer in peers:
        pl.semaphore_signal(barrier, inc=1, device_id={axis: peer}, device_id_type=MESH)
    pl.semaphore_wait(barrier, len(peers))


def grid_peers(n_a, n_b, a, b):
    along_a = [lax.rem(a + da, n_a) * n_b + b for da in range(1, n_a)]
    along_b = [a * n_b + lax.rem(b + db, n_b) for db in range(1, n_b)]
    return along_a, along_b


def send(src, dst, send_sem, recv_sem, axis, peer):
    copy = pltpu.make_async_remote_copy(
        src_ref=src,
        dst_ref=dst,
        send_sem=send_sem,
        recv_sem=recv_sem,
        device_id={axis: peer},
        device_id_type=MESH,
    )
    copy.start()
    return copy


def gather_kernel(axis, n, x_ref, out_ref, a_send, a_recv, b_send, b_recv, own_sem):
    n_a, n_b = factors(n)
    me = lax.axis_index(axis)
    a, b = me // n_b, lax.rem(me, n_b)
    along_a, along_b = grid_peers(n_a, n_b, a, b)
    greet(axis, along_a + along_b)
    a_copies, b_copies = [None], []
    for da in range(1, n_a):
        a_copies.append(
            send(x_ref, out_ref.at[me], a_send.at[da - 1], a_recv.at[da - 1], axis, along_a[da - 1])
        )
    own = pltpu.make_async_copy(x_ref, out_ref.at[me], own_sem)
    own.start()
    for db in range(1, n_b):
        b_copies.append(
            send(x_ref, out_ref.at[me], b_send.at[0, db - 1], b_recv.at[0, db - 1], axis, along_b[db - 1])
        )
    order = sorted(range(1, n_a), key=lambda da: min(da, n_a - da))
    for da in order:
        a_copies[da].wait_recv()
        source = lax.rem(a - da + n_a, n_a) * n_b + b
        for db in range(1, n_b):
            b_copies.append(
                send(
                    out_ref.at[source],
                    out_ref.at[source],
                    b_send.at[da, db - 1],
                    b_recv.at[da, db - 1],
                    axis,
                    along_b[db - 1],
                )
            )
    for copy in b_copies:
        copy.wait()
    for copy in a_copies[1:]:
        copy.wait_send()
    own.wait()


def gather(x, axis, collective_id):
    n = lax.axis_size(axis)
    n_a, n_b = factors(n)
    dma = pltpu.SemaphoreType.DMA
    return pl.pallas_call(
        functools.partial(gather_kernel, axis, n),
        out_shape=jax.ShapeDtypeStruct((n,) + x.shape, x.dtype),
        in_specs=[VM],
        out_specs=VM,
        scratch_shapes=[
            dma((n_a,)),
            dma((n_a,)),
            dma((n_a, n_b)),
            dma((n_a, n_b)),
            dma,
        ],
        name=f"gather{collective_id}",
        compiler_params=pltpu.CompilerParams(collective_id=collective_id, has_side_effects=True),
    )(x)


def scatter_kernel(axis, n, x_ref, out_ref, r1, y, r2, a_send, a_recv, b_send, b_recv):
    n_a, n_b = factors(n)
    me = lax.axis_index(axis)
    a, b = me // n_b, lax.rem(me, n_b)
    along_a, along_b = grid_peers(n_a, n_b, a, b)
    greet(axis, along_a + along_b)
    order = sorted(range(1, n_a), key=lambda da: -min(da, n_a - da)) + [0]
    b_copies, a_copies = {}, []
    for da in order:
        for db in range(1, n_b):
            block = lax.rem(a + da, n_a) * n_b + lax.rem(b + db, n_b)
            b_copies[da, db] = send(
                x_ref.at[block],
                r1.at[da, db - 1],
                b_send.at[da, db - 1],
                b_recv.at[da, db - 1],
                axis,
                along_b[db - 1],
            )

    def arrived(da):
        total = x_ref[lax.rem(a + da, n_a) * n_b + b].astype(jnp.float32)
        for db in range(1, n_b):
            b_copies[da, db].wait_recv()
            total = total + r1[da, db - 1].astype(jnp.float32)
        return total

    for da in order[:-1]:
        y[da - 1] = arrived(da).astype(y.dtype)
        a_copies.append(
            send(y.at[da - 1], r2.at[da - 1], a_send.at[da - 1], a_recv.at[da - 1], axis, along_a[da - 1])
        )
    total = arrived(0)
    for da, copy in zip(order[:-1], a_copies):
        copy.wait_recv()
        total = total + r2[da - 1].astype(jnp.float32)
    out_ref[...] = total.astype(out_ref.dtype)
    for copy in b_copies.values():
        copy.wait_send()
    for copy in a_copies:
        copy.wait_send()


def scatter_sum(x, axis, dtype, collective_id):
    n = lax.axis_size(axis)
    n_a, n_b = factors(n)
    block = x.shape[1:]
    dma = pltpu.SemaphoreType.DMA
    return pl.pallas_call(
        functools.partial(scatter_kernel, axis, n),
        out_shape=jax.ShapeDtypeStruct(block, dtype),
        in_specs=[VM],
        out_specs=VM,
        scratch_shapes=[
            pltpu.VMEM((n_a, n_b - 1) + block, x.dtype),
            pltpu.VMEM((n_a - 1,) + block, x.dtype),
            pltpu.VMEM((n_a - 1,) + block, x.dtype),
            dma((n_a,)),
            dma((n_a,)),
            dma((n_a, n_b)),
            dma((n_a, n_b)),
        ],
        name=f"scatter_sum{collective_id}",
        compiler_params=pltpu.CompilerParams(collective_id=collective_id, has_side_effects=True),
    )(x)


def exchange_kernel(axis, n, x_ref, out_ref, send_sem, recv_sem, own_sem):
    me = lax.axis_index(axis)
    peers = [lax.rem(me + d, n) for d in range(1, n)]
    greet(axis, peers)
    copies = [
        send(x_ref.at[peer], out_ref.at[me], send_sem.at[i], recv_sem.at[i], axis, peer)
        for i, peer in enumerate(peers)
    ]
    own = pltpu.make_async_copy(x_ref.at[me], out_ref.at[me], own_sem)
    own.start()
    for copy in copies:
        copy.wait()
    own.wait()


def exchange(x, axis, collective_id):
    n = lax.axis_size(axis)
    dma = pltpu.SemaphoreType.DMA
    return pl.pallas_call(
        functools.partial(exchange_kernel, axis, n),
        out_shape=jax.ShapeDtypeStruct(x.shape, x.dtype),
        in_specs=[VM],
        out_specs=VM,
        scratch_shapes=[dma((n,)), dma((n,)), dma],
        name=f"exchange{collective_id}",
        compiler_params=pltpu.CompilerParams(collective_id=collective_id, has_side_effects=True),
    )(x)


def hidden_kernel(axis, n, gu_ref, h_ref, r1, y, r2, own_h, b_send, b_recv, a_send, a_recv, ga_send, ga_recv, gb_send, gb_recv, own_sem):
    n_a, n_b = factors(n)
    chunks = gu_ref.shape[0]
    width = gu_ref.shape[3] // n
    me = lax.axis_index(axis)
    a, b = me // n_b, lax.rem(me, n_b)
    along_a, along_b = grid_peers(n_a, n_b, a, b)

    def lanes(owner):
        return pl.ds(pl.multiple_of(owner * width, width), width)

    greet(axis, along_a + along_b)
    order = sorted(range(1, n_a), key=lambda da: -min(da, n_a - da)) + [0]
    b_copies, a_copies, ga, gb, local = {}, {}, {}, [], []
    for c in range(chunks):
        for da in order:
            for db in range(1, n_b):
                block = lax.rem(a + da, n_a) * n_b + lax.rem(b + db, n_b)
                b_copies[c, da, db] = send(
                    gu_ref.at[c, :, :, lanes(block)],
                    r1.at[c, da, db - 1],
                    b_send.at[c, da, db - 1],
                    b_recv.at[c, da, db - 1],
                    axis,
                    along_b[db - 1],
                )

    def arrived(c, da):
        block = lax.rem(a + da, n_a) * n_b + b
        total = gu_ref[c, :, :, lanes(block)].astype(jnp.float32)
        for db in range(1, n_b):
            b_copies[c, da, db].wait_recv()
            total = total + r1[c, da, db - 1].astype(jnp.float32)
        return total

    for c in range(chunks):
        for da in order[:-1]:
            y[c, da - 1] = arrived(c, da).astype(y.dtype)
            a_copies[c, da] = send(
                y.at[c, da - 1],
                r2.at[c, da - 1],
                a_send.at[c, da - 1],
                a_recv.at[c, da - 1],
                axis,
                along_a[da - 1],
            )

    def relay(c):
        for da in sorted(range(1, n_a), key=lambda da: min(da, n_a - da)):
            ga[c, da].wait_recv()
            source = h_ref.at[c, :, lanes(lax.rem(a - da + n_a, n_a) * n_b + b)]
            for db in range(1, n_b):
                gb.append(
                    send(source, source, gb_send.at[c, da, db - 1], gb_recv.at[c, da, db - 1], axis, along_b[db - 1])
                )

    for c in range(chunks):
        total = arrived(c, 0)
        for da in order[:-1]:
            a_copies[c, da].wait_recv()
            total = total + r2[c, da - 1].astype(jnp.float32)
        own_h[c] = (jax.nn.silu(total[0]) * total[1]).astype(own_h.dtype)
        target = h_ref.at[c, :, lanes(me)]
        for da in order[:-1]:
            ga[c, da] = send(own_h.at[c], target, ga_send.at[c, da - 1], ga_recv.at[c, da - 1], axis, along_a[da - 1])
        for db in range(1, n_b):
            gb.append(send(own_h.at[c], target, gb_send.at[c, 0, db - 1], gb_recv.at[c, 0, db - 1], axis, along_b[db - 1]))
        copy = pltpu.make_async_copy(own_h.at[c], target, own_sem.at[c])
        copy.start()
        local.append(copy)
    for c in range(chunks):
        relay(c)
    for copy in gb:
        copy.wait()
    for copy in list(b_copies.values()) + list(a_copies.values()) + list(ga.values()):
        copy.wait_send()
    for copy in local:
        copy.wait()


def hidden_values(gu, axis, collective_id):
    n = lax.axis_size(axis)
    n_a, n_b = factors(n)
    chunks, _, rows, tokens = gu.shape
    width = tokens // n
    dma = pltpu.SemaphoreType.DMA
    pair = (2, rows, width)
    return pl.pallas_call(
        functools.partial(hidden_kernel, axis, n),
        out_shape=jax.ShapeDtypeStruct((chunks, rows, tokens), gu.dtype),
        in_specs=[VM],
        out_specs=VM,
        scratch_shapes=[
            pltpu.VMEM((chunks, n_a, n_b - 1) + pair, gu.dtype),
            pltpu.VMEM((chunks, n_a - 1) + pair, gu.dtype),
            pltpu.VMEM((chunks, n_a - 1) + pair, gu.dtype),
            pltpu.VMEM((chunks, rows, width), gu.dtype),
            dma((chunks, n_a, n_b)),
            dma((chunks, n_a, n_b)),
            dma((chunks, n_a)),
            dma((chunks, n_a)),
            dma((chunks, n_a)),
            dma((chunks, n_a)),
            dma((chunks, n_a, n_b)),
            dma((chunks, n_a, n_b)),
            dma((chunks,)),
        ],
        name="hidden",
        compiler_params=pltpu.CompilerParams(
            collective_id=collective_id, has_side_effects=True, vmem_limit_bytes=67_000_000
        ),
    )(gu)


def chunk_count(rows):
    for count in (7, 6, 4, 3, 2):
        if rows % (count * 8) == 0:
            return count
    return 1


def layer_norm(values, gain):
    mean = jnp.mean(values, axis=-1, keepdims=True)
    centered = values - mean
    variance = jnp.mean(centered * centered, axis=-1, keepdims=True)
    return centered * lax.rsqrt(variance + 1e-06) * gain


def image_ids(lengths, count):
    image_ends = jnp.cumsum(lengths) * 4
    patch_index = jnp.arange(count, dtype=jnp.int32)
    return jnp.sum((patch_index[:, None] >= image_ends[None, :]).astype(jnp.int32), axis=1)


def attend(query, keys, values, image_index):
    scores = jnp.einsum("qhe,khe->hqk", query, keys, preferred_element_type=jnp.float32) * HD ** (
        -0.5
    )
    same_image = image_index[:, None] == image_index[None, :]
    scores = jnp.where(same_image[None], scores, -1e30)
    top = jnp.max(scores, axis=-1, keepdims=True)
    expo = jnp.exp(scores - top)
    weights = (expo / jnp.sum(expo, axis=-1, keepdims=True)).astype(jnp.bfloat16)
    output = jnp.einsum("hqk,khe->qhe", weights, values, preferred_element_type=jnp.float32)
    return output.astype(jnp.bfloat16)


def local(
    vit_input,
    image_lengths,
    positions,
    vit_ln_gain,
    w_qkv,
    w_proj,
    merger_ln_gain,
    merger_w1,
    merger_w2,
    norm_gain,
    gate_up_weight,
    down_weight,
):
    tp_size = lax.axis_size("tp")
    own_patches = vit_input.shape[0]
    patch_width = vit_input.shape[1]
    head_cols = w_qkv.shape[2]
    local_heads = head_cols // HD
    normed_patches = layer_norm(vit_input.astype(jnp.float32), vit_ln_gain).astype(jnp.bfloat16)
    w_qkv_flat = w_qkv.reshape(patch_width, 3 * head_cols)
    projected = jnp.dot(
        gather(normed_patches, "tp", 0).reshape(tp_size * own_patches, patch_width),
        w_qkv_flat,
        preferred_element_type=jnp.float32,
    ).astype(jnp.bfloat16)
    group_patches = projected.shape[0]
    projected = projected.reshape(group_patches, 3, local_heads, HD)
    image_index = image_ids(image_lengths[0], group_patches)
    attended = attend(projected[:, 0], projected[:, 1], projected[:, 2], image_index).reshape(
        group_patches, head_cols
    )
    attn_part = jnp.dot(attended, w_proj, preferred_element_type=jnp.float32).astype(jnp.bfloat16)
    attn_sum = scatter_sum(
        attn_part.reshape(tp_size, own_patches, patch_width), "tp", jnp.float32, 1
    )
    vit_out = vit_input.astype(jnp.float32) + attn_sum
    own_tokens = own_patches // 4
    merged_in = (
        layer_norm(vit_out, merger_ln_gain)
        .astype(jnp.bfloat16)
        .reshape(own_tokens, 4 * patch_width)
    )
    expanded = jax.nn.gelu(
        jnp.dot(
            gather(merged_in, "tp", 2).reshape(tp_size * own_tokens, 4 * patch_width),
            merger_w1,
            preferred_element_type=jnp.float32,
        ),
        approximate=False,
    ).astype(jnp.bfloat16)
    vis_part = jnp.dot(expanded, merger_w2, preferred_element_type=jnp.float32).astype(jnp.bfloat16)
    model_width = merger_w2.shape[1]
    vis_rows = scatter_sum(
        vis_part.reshape(tp_size, own_tokens, model_width), "tp", jnp.bfloat16, 3
    )
    seq_size = lax.axis_size("seq")
    slice_width = model_width // seq_size
    vis_values = vis_rows.astype(jnp.float32)
    row_squares = jnp.sum(vis_values * vis_values, axis=1, keepdims=True)
    inverse = lax.rsqrt(row_squares / D + 1e-06)
    high = inverse.astype(jnp.bfloat16).astype(jnp.float32)
    middle = (inverse - high).astype(jnp.bfloat16).astype(jnp.float32)
    lane = lax.broadcasted_iota(jnp.int32, (own_tokens, 128), 1)
    tail = jnp.where(
        lane == 0, high, jnp.where(lane == 1, middle, jnp.where(lane == 2, inverse - high - middle, 0.0))
    ).astype(jnp.bfloat16)
    payload = jnp.stack(
        [
            jnp.concatenate([vis_rows[:, s * slice_width : (s + 1) * slice_width], tail], axis=1)
            for s in range(seq_size)
        ]
    )
    own_slice = exchange(payload, "seq", 4)
    own_slice = own_slice.reshape(seq_size * own_tokens, slice_width + 128)
    seq_rows = tp_size * seq_size * own_tokens
    all_tokens = gather(own_slice, "tp", 5).reshape(seq_rows, slice_width + 128)
    slots = positions.reshape(seq_size, tp_size, own_tokens).transpose(1, 0, 2).reshape(seq_rows)
    row = lax.broadcasted_iota(jnp.int32, (seq_rows, seq_rows), 0)
    pick = (row == slots[None, :]).astype(jnp.bfloat16)
    ordered = jnp.dot(pick, all_tokens, preferred_element_type=jnp.float32)
    token_values = ordered[:, :slice_width]
    inverse_rms = jnp.sum(ordered[:, slice_width : slice_width + 3], axis=1, keepdims=True)
    normed = (token_values * inverse_rms * norm_gain).astype(jnp.bfloat16)
    hidden_width = gate_up_weight.shape[2]
    weight_rows = gate_up_weight.transpose(1, 2, 0).reshape(2 * hidden_width, slice_width)
    chunks = chunk_count(hidden_width)
    gate_up = lax.dot_general(
        weight_rows, normed, (((1,), (1,)), ((), ())), preferred_element_type=jnp.float32
    ).astype(jnp.bfloat16)
    gate_up = gate_up.reshape(2, chunks, hidden_width // chunks, seq_rows).transpose(1, 0, 2, 3)
    hidden = hidden_values(gate_up, "seq", 6).reshape(hidden_width, seq_rows)
    terms = lax.dot_general(
        hidden, down_weight, (((0,), (0,)), ((), ())), preferred_element_type=jnp.float32
    ).astype(jnp.bfloat16)
    out_rows = seq_rows // tp_size
    down_sum = scatter_sum(terms.reshape(tp_size, out_rows, slice_width), "tp", jnp.float32, 7)
    residual = lax.dynamic_slice_in_dim(token_values, lax.axis_index("tp") * out_rows, out_rows, 0)
    return (residual + down_sum).astype(jnp.bfloat16)


def solution(mesh):
    return jax.shard_map(
        local,
        mesh=mesh,
        in_specs=(
            P(("seq", "tp"), None),
            P("seq", None),
            P(),
            P(),
            P(None, None, "tp"),
            P("tp", None),
            P(),
            P(None, "tp"),
            P("tp", None),
            P("seq"),
            P("seq", None, "tp"),
            P("tp", "seq"),
        ),
        out_specs=P("tp", "seq"),
        check_vma=False,
    )
```

time: 575 us -> 348 us (0.61)
  waiting for transfers between devices: 455 us -> 0 us
  Pallas kernels: 0 us -> 270 us
  local copies, waits for them, and re-layouts: 23.8 us -> 8.95 us
  between operations: 13.7 us -> 0.26 us
  blocking collectives: 5.94 us -> 0 us
    pallas_call x0 -> x8, Pallas kernels: none -> 270 us  [the longest x3 110 us: scatter_sum(): pl.pallas_call(functools.partial(scatter_kernel, axis, n), out_shape=jax....]
    reduce_scatter x3 -> x0, waiting for transfers between devices: 199 us -> none  [the longest x1 68.1 us: local(): lax.psum_scatter(jnp.dot(picked, merger_w2, preferred_element_type=jnp.fl...]
    all_gather x4 -> x0, waiting for transfers between devices: 167 us -> none  [the longest x1 50.2 us: local(): group_rows = lax.all_gather(vis_rows, 'tp', axis=0, tiled=True)]
    unnamed x9 -> x0, waiting for transfers between devices: 66.1 us -> none
    all_to_all x1 -> x0, waiting for transfers between devices: 23.1 us -> none  [local(): lax.all_to_all(group_rows, 'seq', split_axis=1, concat_axis=0, tiled=True)]
    unnamed x18 -> x10, local copies, waits for them, and re-layouts: 14.1 us -> 0.03 us
    psum x1 -> x0, blocking collectives: 5.94 us -> none  [local(): row_squares = lax.psum(jnp.sum(token_values * token_values, axis=1), 'seq')]
    dot_general x5 -> x6, matrix products: 51.9 us -> 53.2 us  [the longest x1 21.4 us: local(): lax.dot_general(weight_rows, normed, (((1,), (1,)), ((), ())), preferred_...]
  transfers between devices with their start and end apart: 9 -> 0, of which waited for: 9 -> 0; matrix products, arithmetic and copies ran while one was open for 1% -> 0% of each run, Pallas kernels for 0% -> 0%
where the time goes in v1:
time: 348 us; the launch traced here: 347 us
  Pallas kernels  270 us (78%)
  matrix products  55.4 us (16%)
  other arithmetic  12.6 us (4%)
  local copies, waits for them, and re-layouts  8.95 us (3%)
    pallas_call x3, Pallas kernels, scatter_sum(): pl.pallas_call(functools.partial(scatter_kernel, axis, n), out_shape=jax....  110 us
    pallas_call x3, Pallas kernels, gather(): pl.pallas_call(functools.partial(gather_kernel, axis, n), out_shape=jax.S...  80.9 us
    pallas_call x1, Pallas kernels, hidden_values(): pl.pallas_call(functools.partial(hidden_kernel, axis, n), out_shape=jax.S...  73 us
    dot_general x1, matrix products, local(): lax.dot_general(weight_rows, normed, (((1,), (1,)), ((), ())), preferred_...  21.4 us
    dot_general x1, matrix products, local(): lax.dot_general(hidden, down_weight, (((0,), (0,)), ((), ())), preferred_...  13.8 us
    dot_general x1, matrix products, local(): jnp.dot(expanded, merger_w2, preferred_element_type=jnp.float32)  11.2 us

profile of v1, /device:TPU:0, one launch (start us, length us, event | category | flops | bytes accessed | tf_op | source)
XLA Modules:
  0.0 347.5 jit_solution(7082641457963880750)
XLA Ops:
  0.0 0.0 copy-start.3
  0.0 0.9 reduce-window.8
  0.9 1.0 convert_reduce_fusion
  2.0 1.1 fusion.11
  3.2 0.1 fusion.63
  3.2 0.8 reshape.154
  4.0 0.1 eq.48
  4.1 1.7 fusion.13.x_ref
  5.8 0.2 broadcast_compare_fusion
  6.0 25.7 %gather0.1 = bf16[8,64,1280]{2,1,0:T(8,128)(2,1)} custom-call(bf16[64,1280]{1,0:T(8,128)(2,1)} %fusion.13.x_ref), custom_call_target="tpu_custom_call" | custom-call | tf_op jit(solution)/shard_map/gather0/pallas_call | solution.py:90
  31.7 0.0 copy-done.3
  31.7 2.1 convolution_convert_fusion.4
  33.9 1.0 fusion.105
  34.8 0.0 copy-start.1
  34.9 1.2 convolution_convert_fusion.5
  36.1 0.0 copy-start
  36.1 0.0 copy-done.1
  36.1 0.0 copy-start.2
  36.1 1.6 convolution_convert_fusion.2
  37.7 27.2 %scatter_sum1.1 = f32[64,1280]{1,0:T(8,128)} custom-call(bf16[8,64,1280]{2,1,0:T(8,128)(2,1)} %bitcast.75), custom_call_target="tpu_custom_call" | custom-call | tf_op jit(solution)/shard_map/scatter_sum1/pallas_call | solution.py:155
  64.9 0.0 copy-done
  64.9 1.1 fusion.58
  66.0 1.2 multiply_reduce_fusion.1
  67.2 0.0 copy-done.2
  67.2 1.1 multiply_convert_fusion.2
  68.3 0.8 reshape.161.x_ref
  69.1 21.8 %gather2.1 = bf16[8,16,5120]{2,1,0:T(8,128)(2,1)} custom-call(bf16[16,5120]{1,0:T(8,128)(2,1)} %reshape.161.x_ref), custom_call_target="tpu_custom_call" | custom-call | tf_op jit(solution)/shard_map/gather2/pallas_call | solution.py:90
  91.0 11.2 %convolution_convert_fusion.1 = bf16[128,8192]{1,0:T(8,128)(2,1)} fusion(bf16[640,8192]{1,0:T(8,128)(2,1)} %param.20, bf16[128,5120]{1,0:T(8,128)(2,1)} %bitcast.80, bf16[5120,640]{1,0:T(8,128)(2,1)} %param.19), kind=kOutput, calls=%fused_computation.2 | convolution fusion | flops 2187411456 | bytes 20447232 | tf_op jit(solution)/shard_map/dot_general | solution.py:401
  102.2 36.3 %scatter_sum3.1 = bf16[16,8192]{1,0:T(8,128)(2,1)} custom-call(bf16[8,16,8192]{2,1,0:T(8,128)(2,1)} %bitcast.78), custom_call_target="tpu_custom_call" | custom-call | tf_op jit(solution)/shard_map/scatter_sum3/pallas_call | solution.py:155
  138.4 1.1 multiply_reduce_fusion
  139.6 1.0 fusion.104
  140.5 0.1 select_convert_fusion
  140.6 0.8 pad_maximum_fusion.x_ref
  141.4 6.8 %exchange4.1 = bf16[4,16,2176]{2,1,0:T(8,128)(2,1)} custom-call(bf16[4,16,2176]{2,1,0:T(8,128)(2,1)} %pad_maximum_fusion.x_ref), custom_call_target="tpu_custom_call" | custom-call | tf_op jit(solution)/shard_map/exchange4/pallas_call | solution.py:192
  148.2 33.4 %gather5.1 = bf16[8,64,2176]{2,1,0:T(8,128)(2,1)} custom-call(bf16[64,2176]{1,0:T(8,128)(2,1)} %bitcast.81), custom_call_target="tpu_custom_call" | custom-call | tf_op jit(solution)/shard_map/gather5/pallas_call | solution.py:90
  181.6 3.0 fusion.6
  184.6 0.1 slice_reduce_fusion
  184.8 0.0 copy-start.4
  184.8 2.6 slice.39
  187.4 0.0 copy-done.4
  187.4 21.4 %convolution_convert_fusion = bf16[512,7392]{0,1:T(8,128)(2,1)S(1)} fusion(bf16[7392,2048]{1,0:T(8,128)(2,1)} %bitcast.84, f32[2048]{0:T(1024)S(1)} %copy-done.4, f32[512]{0:T(512)S(1)} %slice_reduce_fusion, f32[512,2176]{1,0:T(8,128)S(1)} %fusion.6), kind=kOutput, calls=%fused_computation.1 | convolution fusion | flops 15509078016 | bytes 42051584 | tf_op jit(solution)/shard_map/dot_general | solution.py:437
  208.8 3.7 %copy.24 = bf16[2,7,528,512]{3,2,0,1:T(8,128)(2,1)} copy(bf16[2,7,528,512]{3,2,1,0:T(8,128)(2,1)S(1)} %bitcast.74) | data formatting | bytes 15138816 | tf_op jit(solution)/shard_map/reshape | solution.py:440
  212.6 73.0 %hidden.1 = bf16[7,528,512]{2,1,0:T(8,128)(2,1)} custom-call(bf16[7,2,528,512]{3,2,1,0:T(8,128)(2,1)} %bitcast.72), custom_call_target="tpu_custom_call" | custom-call | tf_op jit(solution)/shard_map/hidden/pallas_call | solution.py:290
  285.6 13.8 %convolution_convert_fusion.3 = bf16[512,2048]{1,0:T(8,128)(2,1)} fusion(bf16[3696,512]{1,0:T(8,128)(2,1)} %bitcast.76, bf16[3696,2048]{1,0:T(8,128)(2,1)} %param.23), kind=kOutput, calls=%fused_computation.6 | convolution fusion | flops 7752122368 | bytes 21020672 | tf_op jit(solution)/shard_map/dot_general | solution.py:442
  299.3 46.1 %scatter_sum7.1 = f32[64,2048]{1,0:T(8,128)} custom-call(bf16[8,64,2048]{2,1,0:T(8,128)(2,1)} %bitcast.77), custom_call_target="tpu_custom_call" | custom-call | tf_op jit(solution)/shard_map/scatter_sum7/pallas_call | solution.py:155
  345.5 2.0 add_convert_fusion
  (11 shorter events, 0.1 us)
Async XLA Ops:
  0.0 31.7 %copy-start.3 = (bf16[1280,3,160]{0,2,1:T(8,128)(2,1)S(1)}, bf16[1280,3,160]{0,2,1:T(8,128)(2,1)}, u32[]{:S(2)}) copy-start(bf16[1280,3,160]{0,2,1:T(8,128)(2,1)} %param.16) | copy-start | bytes 3686404
  34.8 1.3 copy-start.1
  36.1 28.8 %copy-start = (bf16[64,1280]{1,0:T(8,128)(2,1)S(1)}, bf16[64,1280]{1,0:T(8,128)(2,1)}, u32[]{:S(2)}) copy-start(bf16[64,1280]{1,0:T(8,128)(2,1)} %param.12) | copy-start | bytes 491524
  36.1 31.1 %copy-start.2 = (f32[1280]{0:T(1024)S(1)}, f32[1280]{0:T(1024)}, u32[]{:S(2)}) copy-start(f32[1280]{0:T(1024)} %param.18) | copy-start | bytes 15364
  184.8 2.6 copy-start.4
